TPU v7x, 512 devices: a whole 4x8x8 slice. The times are simulated.
512 devices in a mesh: dp: 8 (over z_hi, core), mp: 64 (over z_lo, x, y).
Axes of the slice: x: 4, y: 8, z: 8 (z_hi: 4, z_lo: 2; z = z_hi * 2 + z_lo), core: 2. Of those that a mesh axis runs over, the one named last changes fastest.
Arguments:
- inputs: bfloat16 [2048, 4096], P('dp'), may hold values from -6 to 6
- upstream: bfloat16 [2048, 4096], P('dp'), may hold values from -6 to 6
- eig_tiles: bfloat16 [64, 8, 2, 128, 128], P('mp'), may hold values from -0.09375 to 0.09375
- eigvals: float32 [4096], replicated, may hold values from 0.25 to 4
Outputs:
- grad_t: bfloat16 [4096, 2048], P('mp', 'dp')
All inputs are finite; a program needn't handle non-finite values.
Results may differ from a plain program's by a relative error of at most 0.013.
Values may be sent and summed in bfloat16 or wider, within the bound.
No kernel may reach another device: no remote copies, remote signals or barrier semaphores. Data moves between devices by JAX's collectives and lax.ppermute only.
A program may use at most 64 MiB of HBM per device.

v0:
```python
import jax
import jax.numpy as jnp
from jax import lax
from jax.sharding import PartitionSpec as P


def split_up(value, dim, length):
    dims = value.shape
    blocks = value.reshape(*dims[:dim], length, dims[dim] // length, *dims[dim + 1 :])
    return jnp.moveaxis(blocks, dim, 0)


def summed_on_arrival(value, axis, dim):
    length = lax.axis_size(axis)
    blocks = lax.all_to_all(split_up(value, dim, length), axis, 0, 0, tiled=True)
    return jnp.sum(blocks.astype(jnp.float32), axis=0)


def laid_out(blocks, dim):
    blocks = jnp.moveaxis(blocks, 0, dim)
    dims = blocks.shape
    return blocks.reshape(*dims[:dim], dims[dim] * dims[dim + 1], *dims[dim + 2 :])


def copy_for_each(value, axis):
    length = lax.axis_size(axis)
    return lax.all_to_all(
        jnp.broadcast_to(value[None], (length, *value.shape)), axis, 0, 0, tiled=True
    )


def gather_directly(value, axis, dim):
    return laid_out(copy_for_each(value, axis), dim)


def kernel_of(left, right):
    root_left = jnp.sqrt(left)[:, None]
    root_right = jnp.sqrt(right)[None, :]
    return -1.0 / (root_left * root_right * (root_left + root_right))


def on_device(inputs, upstream, eig_tiles, eigvals):
    groups = lax.axis_size("mp")
    member = lax.axis_index("mp")
    width = eigvals.shape[0]
    slab = width // groups
    tile_rows = eig_tiles.shape[1]
    tile_cols = eig_tiles.shape[2]
    tile = eig_tiles.shape[3]
    grid_rows = width // (tile_rows * tile)
    grid_cols = groups // grid_rows
    piece = tile_cols * tile // groups
    local = jnp.transpose(eig_tiles[0], (0, 2, 1, 3)).reshape(tile_rows * tile, groups, piece)
    moved = lax.all_to_all(local, "mp", split_axis=1, concat_axis=1, tiled=True)
    moved = moved.reshape(tile_rows, tile, grid_rows, grid_cols, piece)
    basis = jnp.transpose(moved, (0, 2, 1, 3, 4)).reshape(width, slab)
    ordered = jnp.transpose(eigvals.reshape(tile_cols, grid_cols, tile), (1, 0, 2)).reshape(
        grid_cols, groups, piece
    )
    ordered = jnp.transpose(ordered, (1, 0, 2)).reshape(width)
    own = lax.dynamic_slice_in_dim(ordered, member * slab, slab)
    proj_in = jnp.dot(inputs, basis, preferred_element_type=jnp.float32).astype(jnp.bfloat16)
    proj_up = jnp.dot(upstream, basis, preferred_element_type=jnp.float32).astype(jnp.bfloat16)
    stacked = jnp.stack([proj_in, proj_up], 0)
    over_tokens = (((0,), (0,)), ((), ()))
    pieces = lax.all_gather(stacked, "mp", axis=2, tiled=True)
    part_in = pieces[0]
    part_up = pieces[1]
    block = lax.dot_general(proj_in, part_up, over_tokens, preferred_element_type=jnp.float32)
    block = block + lax.dot_general(
        proj_up, part_in, over_tokens, preferred_element_type=jnp.float32
    )
    joined = jnp.concatenate([block, part_in.astype(jnp.float32)], 0)
    gram = joined[:slab]
    all_in = joined[slab:].astype(jnp.bfloat16)
    share = summed_on_arrival(gram.astype(jnp.bfloat16), "dp", 0)
    count = share.shape[0]
    own_part = lax.dynamic_slice_in_dim(own, lax.axis_index("dp") * count, count)
    part = (kernel_of(own_part, ordered) * (0.5 * share)).astype(jnp.bfloat16)
    weighted = gather_directly(part, "dp", 0)
    over_columns = (((1,), (1,)), ((), ()))
    mixed = lax.dot_general(all_in, weighted, over_columns, preferred_element_type=jnp.float32)
    factor = 2.0 / (lax.axis_size("dp") * inputs.shape[0])
    update = (proj_up.astype(jnp.float32) / jnp.sqrt(own)[None, :] + factor * mixed).astype(
        jnp.bfloat16
    )
    own_rows = lax.all_to_all(basis, "mp", split_axis=0, concat_axis=1, tiled=True)
    every_update = gather_directly(update, "mp", 1)
    result = lax.dot_general(
        own_rows, every_update, over_columns, preferred_element_type=jnp.float32
    )
    return result.astype(jnp.bfloat16)


def solution(mesh):
    return jax.shard_map(
        on_device,
        mesh=mesh,
        in_specs=(P("dp", None), P("dp", None), P("mp", None, None, None, None), P()),
        out_specs=P("mp", "dp"),
        check_vma=False,
    )
```

profile of v0, /device:TPU:8, one launch (start us, length us, event | category | flops | bytes accessed | tf_op | source)
XLA Modules:
  0.0 494.4 jit_solution(2258323800576001424)
XLA Ops:
  6.5 1.5 copy.11
  8.0 0.1 reshape.93
  8.2 30.6 %all_to_all.36 = bf16[1024,64,4]{0,2,1:T(4,128)(2,1)S(1)} all-to-all(bf16[1024,64,4]{0,2,1:T(4,128)(2,1)S(1)} %reshape.93), channel_id=1, replica_groups=mesh['dp'=8,'mp'=64] {'mp'}, dimensions={1} | all-to-all | bytes 1048576 | tf_op jit(solution)/shard_map/all_to_all | solution.py:54
  38.7 1.0 reshape.102
  39.7 1.7 copy.13
  41.4 0.4 reshape.95
  41.8 0.8 convolution_convert_fusion.1
  42.6 0.8 copy-done.1
  43.4 0.8 convolution_convert_fusion
  44.2 0.6 pad_maximum_fusion
  44.8 303.2 %all-gather.2.cloned.1.call-done = bf16[2,256,4096]{1,2,0:T(8,128)(2,1)} async-done(((bf16[2,256,64]{1,2,0:T(8,128)(2,1)}), bf16[2,256,4096]{1,2,0:T(8,128)(2,1)}) %all-gather.2.cloned.1.call-update) | async-done | bytes 4194320 | tf_op jit(solution)/shard_map/all_gather | solution.py:66
  348.1 2.3 fusion.2
  350.4 3.2 fusion.1
  353.6 6.8 %all-to-all-start.1 = ((bf16[8,8,4096]{2,1,0:T(8,128)(2,1)}), bf16[8,8,4096]{2,1,0:T(8,128)(2,1)S(1)}, u32[]{:S(2)}, u32[]{:S(2)}) async-start(bf16[8,8,4096]{2,1,0:T(8,128)(2,1)} %fusion.1), calls=%async_computation.1 | async-start | bytes 1048576 | tf_op jit(solution)/shard_map/all_to_all | solution.py:15
  360.5 1.2 copy.15
  361.8 1.3 reshape.98
  363.2 15.2 %all-to-all-done.1 = bf16[8,8,4096]{2,1,0:T(8,128)(2,1)S(1)} async-done(((bf16[8,8,4096]{2,1,0:T(8,128)(2,1)}), bf16[8,8,4096]{2,1,0:T(8,128)(2,1)S(1)}, u32[]{:S(2)}, u32[]{:S(2)}) %all-to-all-start.1) | async-done | bytes 524320 | tf_op jit(solution)/shard_map/all_to_all | solution.py:15
  378.5 0.1 multiply_convert_fusion
  378.6 0.9 broadcast_in_dim.4
  379.4 3.5 all-to-all-start.2
  382.9 1.4 all_to_all.28
  384.3 2.9 copy.17
  387.3 3.0 reshape.103
  390.3 10.5 %all-to-all-done.2 = bf16[8,8,4096]{2,1,0:T(8,128)(2,1)S(1)} async-done(((bf16[8,8,4096]{2,1,0:T(8,128)(2,1)}), bf16[8,8,4096]{2,1,0:T(8,128)(2,1)S(1)}, u32[]{:S(2)}, u32[]{:S(2)}) %all-to-all-start.2) | async-done | bytes 524320 | tf_op jit(solution)/shard_map/all_to_all | solution.py:27
  400.8 8.2 %all-to-all-start.4 = ((bf16[64,2,2048]{2,1,0:T(2,128)(2,1)}), bf16[64,2,2048]{2,1,0:T(2,128)(2,1)S(1)}, u32[]{:S(2)}, u32[]{:S(2)}) async-start(bf16[64,2,2048]{2,1,0:T(2,128)(2,1)} %reshape.103), calls=%async_computation.4 | async-start | bytes 1048576 | tf_op jit(solution)/shard_map/all_to_all | solution.py:87
  409.1 2.1 fusion.11
  411.2 15.7 %all-to-all-done.4 = bf16[64,2,2048]{2,1,0:T(2,128)(2,1)S(1)} async-done(((bf16[64,2,2048]{2,1,0:T(2,128)(2,1)}), bf16[64,2,2048]{2,1,0:T(2,128)(2,1)S(1)}, u32[]{:S(2)}, u32[]{:S(2)}) %all-to-all-start.4) | async-done | bytes 524320 | tf_op jit(solution)/shard_map/all_to_all | solution.py:87
  426.9 1.6 broadcast_in_dim.5
  428.4 5.7 %all-to-all-start.3 = ((bf16[64,256,64]{1,2,0:T(8,128)(2,1)}), bf16[64,256,64]{1,2,0:T(8,128)(2,1)}, u32[]{:S(2)}, u32[]{:S(2)}) async-start(bf16[64,256,64]{1,2,0:T(8,128)(2,1)} %broadcast_in_dim.5), calls=%async_computation.3 | async-start | bytes 4194304 | tf_op jit(solution)/shard_map/all_to_all | solution.py:27
  434.2 1.6 reshape.104
  435.8 48.6 %all-to-all-done.3 = bf16[64,256,64]{1,2,0:T(8,128)(2,1)} async-done(((bf16[64,256,64]{1,2,0:T(8,128)(2,1)}), bf16[64,256,64]{1,2,0:T(8,128)(2,1)}, u32[]{:S(2)}, u32[]{:S(2)}) %all-to-all-start.3) | async-done | bytes 2097184 | tf_op jit(solution)/shard_map/all_to_all | solution.py:27
  484.5 3.0 fusion.15
  (12 shorter events, 0.4 us)
Async XLA Ops:
  6.5 35.3 %copy-start = (bf16[256,4096]{1,0:T(8,128)(2,1)S(1)}, bf16[256,4096]{1,0:T(8,128)(2,1)}, u32[]{:S(2)}) copy-start(bf16[256,4096]{1,0:T(8,128)(2,1)} %param.5) | copy-start | bytes 6291460
  6.5 341.5 %all-gather.2.cloned.1.call-start = ((), (), s32[]{:S(2)}) async-start(), calls=%async_computation.5 | async-start | bytes 4259840 | tf_op jit(solution)/shard_map/all_gather | solution.py:66
  41.8 1.6 copy-start.1
  350.4 10.0 %copy-start.2 = (f32[4096]{0:T(1024)S(1)}, f32[4096]{0:T(1024)}, u32[]{:S(2)}) copy-start(f32[4096]{0:T(1024)} %param.7) | copy-start | bytes 49156
  353.6 24.8 %all-to-all-start.1 = ((bf16[8,8,4096]{2,1,0:T(8,128)(2,1)}), bf16[8,8,4096]{2,1,0:T(8,128)(2,1)S(1)}, u32[]{:S(2)}, u32[]{:S(2)}) async-start(bf16[8,8,4096]{2,1,0:T(8,128)(2,1)} %fusion.1), calls=%async_computation.1 | async-start | bytes 1048576 | tf_op jit(solution)/shard_map/all_to_all | solution.py:15
  379.4 21.4 %all-to-all-start.2 = ((bf16[8,8,4096]{2,1,0:T(8,128)(2,1)}), bf16[8,8,4096]{2,1,0:T(8,128)(2,1)S(1)}, u32[]{:S(2)}, u32[]{:S(2)}) async-start(bf16[8,8,4096]{2,1,0:T(8,128)(2,1)} %broadcast_in_dim.4), calls=%async_computation.2 | async-start | bytes 1048576 | tf_op jit(solution)/shard_map/all_to_all | solution.py:27
  400.8 26.1 %all-to-all-start.4 = ((bf16[64,2,2048]{2,1,0:T(2,128)(2,1)}), bf16[64,2,2048]{2,1,0:T(2,128)(2,1)S(1)}, u32[]{:S(2)}, u32[]{:S(2)}) async-start(bf16[64,2,2048]{2,1,0:T(2,128)(2,1)} %reshape.103), calls=%async_computation.4 | async-start | bytes 1048576 | tf_op jit(solution)/shard_map/all_to_all | solution.py:87
  428.4 56.0 %all-to-all-start.3 = ((bf16[64,256,64]{1,2,0:T(8,128)(2,1)}), bf16[64,256,64]{1,2,0:T(8,128)(2,1)}, u32[]{:S(2)}, u32[]{:S(2)}) async-start(bf16[64,256,64]{1,2,0:T(8,128)(2,1)} %broadcast_in_dim.5), calls=%async_computation.3 | async-start | bytes 4194304 | tf_op jit(solution)/shard_map/all_to_all | solution.py:27
Sparse Core Ops, SparseCore 0:
  45.0 303.0 all-gather.1
where the time goes:
time: 495 us; the launch traced here: 494 us
  waiting for transfers between devices  393 us (79%)
  blocking collectives  30.6 us (6%)
  starting transfers between devices  24.3 us (5%)
  local copies, waits for them, and re-layouts  19.8 us (4%)
  between operations  13.5 us (3%)
  matrix products  12.1 us (2%)
    all_gather x1, waiting for transfers between devices, on_device(): pieces = lax.all_gather(stacked, 'mp', axis=2, tiled=True)  303 us
    all_to_all x2, waiting for transfers between devices, copy_for_each(): lax.all_to_all(jnp.broadcast_to(value[None], (length, *value.shape)), axi...  59.2 us
    all_to_all x1, blocking collectives, on_device(): moved = lax.all_to_all(local, 'mp', split_axis=1, concat_axis=1, tiled=True)  30.6 us
    all_to_all x1, waiting for transfers between devices, on_device(): lax.all_to_all(basis, 'mp', split_axis=0, concat_axis=1, tiled=True)  15.7 us
    all_to_all x1, waiting for transfers between devices, summed_on_arrival(): lax.all_to_all(split_up(value, dim, length), axis, 0, 0, tiled=True)  15.2 us
  transfers between devices with their start and end apart: 5, of which 5 were waited for; matrix products, arithmetic and copies ran while one was open for 3% of the time, Pallas kernels for 0%

commit v1 on v0

--- a/solution.py
+++ b/solution.py
@@ -63,7 +63,8 @@
     proj_up = jnp.dot(upstream, basis, preferred_element_type=jnp.float32).astype(jnp.bfloat16)
     stacked = jnp.stack([proj_in, proj_up], 0)
     over_tokens = (((0,), (0,)), ((), ()))
-    pieces = lax.all_gather(stacked, "mp", axis=2, tiled=True)
+    outgoing = jnp.stack([stacked] * lax.axis_size("mp"))
+    pieces = jnp.concatenate(lax.all_to_all(outgoing, "mp", 0, 0), axis=2)
     part_in = pieces[0]
     part_up = pieces[1]
     block = lax.dot_general(proj_in, part_up, over_tokens, preferred_element_type=jnp.float32)

time: 495 us -> 278 us (0.56)
  waiting for transfers between devices: 393 us -> 89.9 us
  blocking collectives: 30.6 us -> 132 us
  between operations: 13.5 us -> 0.15 us
    all_gather x1 -> x0, waiting for transfers between devices: 303 us -> none  [on_device(): pieces = lax.all_gather(stacked, 'mp', axis=2, tiled=True)]
    all_to_all x0 -> x1, blocking collectives: none -> 101 us  [on_device(): pieces = jnp.concatenate(lax.all_to_all(outgoing, 'mp', 0, 0), axis=2)]
  transfers between devices with their start and end apart: 5 -> 4, of which waited for: 5 -> 4; matrix products, arithmetic and copies ran while one was open for 3% -> 4% of each run, Pallas kernels for 0% -> 0%
where the time goes in v1:
time: 278 us; the launch traced here: 277 us
  blocking collectives  132 us (47%)
  waiting for transfers between devices  89.9 us (32%)
  starting transfers between devices  26.1 us (9%)
  local copies, waits for them, and re-layouts  20.4 us (7%)
  matrix products  8.76 us (3%)
    all_to_all x1, blocking collectives, on_device(): pieces = jnp.concatenate(lax.all_to_all(outgoing, 'mp', 0, 0), axis=2)  101 us
    all_to_all x2, waiting for transfers between devices, copy_for_each(): lax.all_to_all(jnp.broadcast_to(value[None], (length, *value.shape)), axi...  59 us
    all_to_all x1, blocking collectives, on_device(): moved = lax.all_to_all(local, 'mp', split_axis=1, concat_axis=1, tiled=True)  30.6 us
    all_to_all x1, waiting for transfers between devices, summed_on_arrival(): lax.all_to_all(split_up(value, dim, length), axis, 0, 0, tiled=True)  15.6 us
    all_to_all x1, waiting for transfers between devices, on_device(): lax.all_to_all(basis, 'mp', split_axis=0, concat_axis=1, tiled=True)  15.4 us
    all_to_all x2, starting transfers between devices, copy_for_each(): lax.all_to_all(jnp.broadcast_to(value[None], (length, *value.shape)), axi...  9.88 us
    all_to_all x1, starting transfers between devices, summed_on_arrival(): lax.all_to_all(split_up(value, dim, length), axis, 0, 0, tiled=True)  9.41 us
    all_to_all x1, starting transfers between devices, on_device(): lax.all_to_all(basis, 'mp', split_axis=0, concat_axis=1, tiled=True)  6.85 us
  transfers between devices with their start and end apart: 4, of which 4 were waited for; matrix products, arithmetic and copies ran while one was open for 4% of the time, Pallas kernels for 0%

profile of v1, /device:TPU:8, one launch (start us, length us, event | category | flops | bytes accessed | tf_op | source)
XLA Modules:
  0.0 277.4 jit_solution(18315996536244757299)
XLA Ops:
  0.0 1.5 copy.19
  1.6 30.6 %all_to_all.41 = bf16[1024,64,4]{0,2,1:T(4,128)(2,1)S(1)} all-to-all(bf16[1024,64,4]{0,2,1:T(4,128)(2,1)S(1)} %reshape.103), channel_id=1, replica_groups=mesh['dp'=8,'mp'=64] {'mp'}, dimensions={1} | all-to-all | bytes 1048576 | tf_op jit(solution)/shard_map/all_to_all | solution.py:54
  32.2 1.0 reshape.113
  33.2 1.7 copy.21
  35.3 0.8 convolution_convert_fusion.1
  36.1 0.8 copy-done.3
  36.9 0.8 convolution_convert_fusion
  37.7 0.5 stack.11
  38.2 101.3 %all_to_all.42 = bf16[64,2,256,64]{2,3,1,0:T(8,128)(2,1)S(1)} all-to-all(bf16[64,2,256,64]{2,3,1,0:T(8,128)(2,1)S(1)} %stack.11), channel_id=1, replica_groups=mesh['dp'=8,'mp'=64] {'mp'}, dimensions={0} | all-to-all | bytes 8388608 | tf_op jit(solution)/shard_map/all_to_all | solution.py:67
  139.4 0.6 copy.31
  140.0 0.5 fusion.17
  140.6 0.7 fusion.18
  141.3 0.6 copy-done.1
  141.9 1.6 fusion.1
  143.5 9.4 %all-to-all-start.2 = ((bf16[8,8,4096]{2,1,0:T(8,128)(2,1)}), bf16[8,8,4096]{2,1,0:T(8,128)(2,1)S(1)}, u32[]{:S(2)}, u32[]{:S(2)}) async-start(bf16[8,8,4096]{2,1,0:T(8,128)(2,1)} %fusion.1), calls=%async_computation.2 | async-start | bytes 1048576 | tf_op jit(solution)/shard_map/all_to_all | solution.py:15
  153.0 1.3 copy.23
  154.2 1.3 reshape.108
  155.6 15.6 %all-to-all-done.2 = bf16[8,8,4096]{2,1,0:T(8,128)(2,1)S(1)} async-done(((bf16[8,8,4096]{2,1,0:T(8,128)(2,1)}), bf16[8,8,4096]{2,1,0:T(8,128)(2,1)S(1)}, u32[]{:S(2)}, u32[]{:S(2)}) %all-to-all-start.2) | async-done | bytes 524320 | tf_op jit(solution)/shard_map/all_to_all | solution.py:15
  171.4 0.8 broadcast_in_dim.4
  172.2 4.1 %all-to-all-start.3 = ((bf16[8,8,4096]{2,1,0:T(8,128)(2,1)}), bf16[8,8,4096]{2,1,0:T(8,128)(2,1)}, u32[]{:S(2)}, u32[]{:S(2)}) async-start(bf16[8,8,4096]{2,1,0:T(8,128)(2,1)} %broadcast_in_dim.4), calls=%async_computation.3 | async-start | bytes 1048576 | tf_op jit(solution)/shard_map/all_to_all | solution.py:27
  176.4 1.4 all_to_all.32
  177.8 2.2 copy.26
  180.0 1.5 reshape.114
  181.5 11.0 %all-to-all-done.3 = bf16[8,8,4096]{2,1,0:T(8,128)(2,1)} async-done(((bf16[8,8,4096]{2,1,0:T(8,128)(2,1)}), bf16[8,8,4096]{2,1,0:T(8,128)(2,1)}, u32[]{:S(2)}, u32[]{:S(2)}) %all-to-all-start.3) | async-done | bytes 524320 | tf_op jit(solution)/shard_map/all_to_all | solution.py:27
  192.6 6.9 %all-to-all-start.5 = ((bf16[64,2,2048]{2,1,0:T(2,128)(2,1)}), bf16[64,2,2048]{2,1,0:T(2,128)(2,1)S(1)}, u32[]{:S(2)}, u32[]{:S(2)}) async-start(bf16[64,2,2048]{2,1,0:T(2,128)(2,1)} %reshape.114), calls=%async_computation.5 | async-start | bytes 1048576 | tf_op jit(solution)/shard_map/all_to_all | solution.py:88
  199.5 2.2 fusion.8
  201.7 15.4 %all-to-all-done.5 = bf16[64,2,2048]{2,1,0:T(2,128)(2,1)S(1)} async-done(((bf16[64,2,2048]{2,1,0:T(2,128)(2,1)}), bf16[64,2,2048]{2,1,0:T(2,128)(2,1)S(1)}, u32[]{:S(2)}, u32[]{:S(2)}) %all-to-all-start.5) | async-done | bytes 524320 | tf_op jit(solution)/shard_map/all_to_all | solution.py:88
  217.1 1.6 broadcast_in_dim.5
  218.7 5.7 %all-to-all-start.4 = ((bf16[64,256,64]{1,2,0:T(8,128)(2,1)}), bf16[64,256,64]{1,2,0:T(8,128)(2,1)}, u32[]{:S(2)}, u32[]{:S(2)}) async-start(bf16[64,256,64]{1,2,0:T(8,128)(2,1)} %broadcast_in_dim.5), calls=%async_computation.4 | async-start | bytes 4194304 | tf_op jit(solution)/shard_map/all_to_all | solution.py:27
  224.4 2.3 reshape.115
  226.7 47.9 %all-to-all-done.4 = bf16[64,256,64]{1,2,0:T(8,128)(2,1)} async-done(((bf16[64,256,64]{1,2,0:T(8,128)(2,1)}), bf16[64,256,64]{1,2,0:T(8,128)(2,1)}, u32[]{:S(2)}, u32[]{:S(2)}) %all-to-all-start.4) | async-done | bytes 2097184 | tf_op jit(solution)/shard_map/all_to_all | solution.py:27
  274.7 2.7 fusion.12
  (17 shorter events, 1.0 us)
Async XLA Ops:
  0.0 35.3 %copy-start = (bf16[256,4096]{1,0:T(8,128)(2,1)S(1)}, bf16[256,4096]{1,0:T(8,128)(2,1)}, u32[]{:S(2)}) copy-start(bf16[256,4096]{1,0:T(8,128)(2,1)} %param.5) | copy-start | bytes 6291460
  35.3 1.6 copy-start.3
  140.6 1.3 copy-start.1
  141.9 11.0 %copy-start.4 = (f32[4096]{0:T(1024)S(1)}, f32[4096]{0:T(1024)}, u32[]{:S(2)}) copy-start(f32[4096]{0:T(1024)} %param.7) | copy-start | bytes 49156
  143.5 27.7 %all-to-all-start.2 = ((bf16[8,8,4096]{2,1,0:T(8,128)(2,1)}), bf16[8,8,4096]{2,1,0:T(8,128)(2,1)S(1)}, u32[]{:S(2)}, u32[]{:S(2)}) async-start(bf16[8,8,4096]{2,1,0:T(8,128)(2,1)} %fusion.1), calls=%async_computation.2 | async-start | bytes 1048576 | tf_op jit(solution)/shard_map/all_to_all | solution.py:15
  172.2 20.3 %all-to-all-start.3 = ((bf16[8,8,4096]{2,1,0:T(8,128)(2,1)}), bf16[8,8,4096]{2,1,0:T(8,128)(2,1)}, u32[]{:S(2)}, u32[]{:S(2)}) async-start(bf16[8,8,4096]{2,1,0:T(8,128)(2,1)} %broadcast_in_dim.4), calls=%async_computation.3 | async-start | bytes 1048576 | tf_op jit(solution)/shard_map/all_to_all | solution.py:27
  192.6 24.6 %all-to-all-start.5 = ((bf16[64,2,2048]{2,1,0:T(2,128)(2,1)}), bf16[64,2,2048]{2,1,0:T(2,128)(2,1)S(1)}, u32[]{:S(2)}, u32[]{:S(2)}) async-start(bf16[64,2,2048]{2,1,0:T(2,128)(2,1)} %reshape.114), calls=%async_computation.5 | async-start | bytes 1048576 | tf_op jit(solution)/shard_map/all_to_all | solution.py:88
  217.1 1.6 copy-start.2
  218.7 56.0 %all-to-all-start.4 = ((bf16[64,256,64]{1,2,0:T(8,128)(2,1)}), bf16[64,256,64]{1,2,0:T(8,128)(2,1)}, u32[]{:S(2)}, u32[]{:S(2)}) async-start(bf16[64,256,64]{1,2,0:T(8,128)(2,1)} %broadcast_in_dim.5), calls=%async_computation.4 | async-start | bytes 4194304 | tf_op jit(solution)/shard_map/all_to_all | solution.py:27
